TPU v7x, 32 devices: a whole 2x2x4 slice. The times are simulated.
32 devices in a mesh: row: 4 (over z), vec: 8 (over y, x, core).
Axes of the slice: x: 2, y: 2, z: 4, core: 2. Of those that a mesh axis runs over, the one named last changes fastest.
Arguments:
- vectors: float32 [4096, 4096], P('row', 'vec'), may hold values from -6 to 6
- block_index: int32 [3, 4], replicated, may hold values from 0 to 7
- block_offset: int32 [3, 4], replicated, may hold values from 0 to 3, as said below
- reflector_vectors: float32 [4, 8, 512, 256], P('row', 'vec'), may hold values from -0.25 to 0.25
- reflector_factors: float32 [4, 8, 256, 256], P('row', 'vec'), may hold values from -0.1875 to 0.1875
Outputs:
- updated: float32 [4096, 4096], P('row', 'vec')
Inputs may be any that keep to these rules, and one draw needn't show every extreme that they name: `block_offset`: the last owner's offset is at most 2, so every block lies inside the slab.
All inputs are finite; a program needn't handle non-finite values.
Results may differ from a plain program's by a relative error of at most 0.0001.
Values sent between devices are 32-bit elements; how exact they have to be, the bound alone decides.
No kernel may reach another device: no remote copies, remote signals or barrier semaphores. Data moves between devices by JAX's collectives and lax.ppermute only.
A program may use at most 64 MiB of HBM per device.

v0:
```python
import jax
import jax.numpy as jnp
from jax import lax
from jax.sharding import PartitionSpec as P

FRONTS = 3


def broadcast(value, axis, source):
    kept = jnp.where(lax.axis_index(axis) == source, value, 0).astype(value.dtype)
    return lax.psum(kept, axis)


def passed_along(value, axis, steps):
    count = lax.axis_size(axis)
    first, last = (max(0, -steps), min(count, count - steps))
    return lax.ppermute(value, axis, [(source, source + steps) for source in range(first, last)])


def apply_reflector_block(row_window, vector_matrix, triangular_matrix):
    high_precision = lax.Precision.HIGHEST
    inner_product = jnp.dot(
        vector_matrix.T, row_window, precision=high_precision, preferred_element_type=jnp.float32
    )
    mixed_rows = jnp.dot(
        jnp.triu(triangular_matrix),
        inner_product,
        precision=high_precision,
        preferred_element_type=jnp.float32,
    )
    return row_window - jnp.dot(
        vector_matrix, mixed_rows, precision=high_precision, preferred_element_type=jnp.float32
    )


def body(vectors, block_index, block_offset, reflector_vectors, reflector_factors):
    rows_here = vectors.shape[0]
    width = reflector_vectors.shape[3]
    span = reflector_vectors.shape[2]
    slots = rows_here // width
    owner_index = lax.axis_index("row")
    local_rows = vectors
    for front in range(FRONTS):
        root_owner = block_index[front, owner_index]
        vector_matrix, triangular_matrix = (
            broadcast(reflector_vectors[0, 0], "vec", root_owner),
            broadcast(reflector_factors[0, 0], "vec", root_owner),
        )
        slot = block_offset[front, owner_index]
        crossing = slot == slots - 1
        lower_rows = passed_along(local_rows[:width], "row", -1)
        bottom_row = local_rows[rows_here - width :]
        edge = lax.cond(
            crossing,
            lambda: apply_reflector_block(
                jnp.concatenate([bottom_row, lower_rows], axis=0), vector_matrix, triangular_matrix
            ),
            lambda: jnp.concatenate([bottom_row, lower_rows], axis=0),
        )
        sent = jnp.where(crossing, edge[width:], lower_rows)
        back = passed_along(sent, "row", 1)
        top_rows = jnp.where(owner_index > 0, back, local_rows[:width])
        local_rows = jnp.concatenate([top_rows, local_rows[width:]], axis=0)
        start_row = jnp.minimum(slot, slots - 2) * width

        def own_window():
            row_window = lax.dynamic_slice_in_dim(local_rows, start_row, span, 0)
            return lax.dynamic_update_slice_in_dim(
                local_rows,
                apply_reflector_block(row_window, vector_matrix, triangular_matrix),
                start_row,
                0,
            )

        def crossed_rows():
            return jnp.concatenate([local_rows[: rows_here - width], edge[:width]], axis=0)

        local_rows = lax.cond(crossing, crossed_rows, own_window)
    return local_rows


def solution(mesh):
    return jax.shard_map(
        body,
        mesh=mesh,
        in_specs=(
            P("row", "vec"),
            P(),
            P(),
            P("row", "vec", None, None),
            P("row", "vec", None, None),
        ),
        out_specs=P("row", "vec"),
        check_vma=False,
    )
```

profile of v0, /device:TPU:12, one launch (start us, length us, event | category | flops | bytes accessed | tf_op | source)
XLA Modules:
  0.0 191.9 jit_solution(16495925374914444277)
XLA Ops:
  6.5 1.5 constant_dynamic-slice_fusion.2
  9.9 2.3 %select_bitcast_fusion = (f32[512,256]{1,0:T(8,128)}, f32[512,256]{1,0:T(8,128)}, f32[512,256]{1,0:T(8,128)}) fusion(f32[1,1,512,256]{3,2,1,0:T(8,128)} %param.20, pred[]{:T(512)S(6)} %eq.26, pred[]{:T(512)S(6)} %eq.24, pred[]{:T(512)S(6)} %eq.25), kind=kLoop, calls=%fused_computation.81 | loop fusion | flops 393216 | bytes 2097155 | tf_op jit(solution)/shard_map/jit(_where)/select_n | solution.py:10
  12.2 0.9 select_bitcast_fusion.3
  13.1 0.9 copy-done.8
  14.3 2.4 %collective-permute-start = (f32[256,512]{0,1:T(8,128)S(1)}, f32[256,512]{0,1:T(8,128)S(1)}, u32[]{:S(2)}, u32[]{:S(2)}) collective-permute-start(f32[256,512]{0,1:T(8,128)S(1)} %copy.15), channel_id=1, source_target_pairs={{8,0},{16,8},{24,16},{9,1},{17,9},{25,17},{10,2},{18,10},{26,18},{... | collective-permute-start | bytes 1572872 | tf_op jit(solution)/shard_map/ppermute | solution.py:17
  17.5 12.4 %collective-permute-done = f32[256,512]{0,1:T(8,128)S(1)} collective-permute-done((f32[256,512]{0,1:T(8,128)S(1)}, f32[256,512]{0,1:T(8,128)S(1)}, u32[]{:S(2)}, u32[]{:S(2)}) %collective-permute-start) | collective-permute-done | bytes 524320 | tf_op jit(solution)/shard_map/ppermute | solution.py:17
  29.9 47.6 %all-reduce.3.cloned.1.call-done = (f32[256,256]{1,0:T(8,128)}, f32[512,256]{1,0:T(8,128)}, f32[256,256]{1,0:T(8,128)}, f32[512,256]{1,0:T(8,128)}, f32[256,256]{1,0:T(8,128)}, /*index=5*/f32[512,256]{1,0:T(8,128)}) async-done(((f32[256,256]{1,0:T(8,128)}, f32[512,256]{1,0:T(8,128)}, f32[256,256]{1,0:T(8,128)}, f32[512,256]{1,0:T(8,128)}, f32[256,256]{1,0:T(8,128)}, /*index=5*/f32[512,256]{1,0:T(8,128)}), ...) | async-done | bytes 2359312 | tf_op jit(solution)/shard_map/psum | solution.py:11
  77.5 6.6 %conditional.6 = (f32[512,512]{0,1:T(8,128)}, f32[256,512]{0,1:T(8,128)S(1)}) conditional(s32[]{:T(128)} %convert_element_type.22, (f32[256,512]{0,1:T(8,128)S(1)}, f32[256,512]{0,1:T(8,128)S(1)}) %tuple.85, (f32[256,512]{0,1:T(8,128)S(1)}, f32[256,512]{0,1:T(8,128)S(1)}, f32[256,256]{1,0:T(8,128)}, f32[512,256]{1,0:T(8,128)}) %tuple.86), branch_computations={%region_2.3_spmd, %region_3.4_spmd} | conditional | flops 2013659392 | bytes 12847176 | solution.py:53
  77.6 0.9 copy-done.4
  78.5 1.0 fusion.49
  80.2 2.9 %fusion = f32[512,512]{0,1:T(8,128)} fusion(f32[512,512]{0,1:T(8,128)S(1)} %constant_dynamic-update-slice_fusion, f32[256,512]{1,0:T(8,128)S(1)} %fusion.1, f32[512,256]{1,0:T(8,128)S(1)} %copy-done.4), kind=kOutput, calls=%fused_computation.2 | convolution fusion | flops 805568512 | bytes 3145728 | tf_op jit(solution)/shard_map/cond/branch_1_fun/dot_general | solution.py:31
  83.0 1.1 slice.120
  84.2 1.9 %collective-permute-start.1 = (f32[256,512]{0,1:T(8,128)S(1)}, f32[256,512]{0,1:T(8,128)S(1)}, u32[]{:S(2)}, u32[]{:S(2)}) collective-permute-start(f32[256,512]{0,1:T(8,128)S(1)} %broadcast_select_fusion), channel_id=1, source_target_pairs={{0,8},{8,16},{16,24},{1,9},{9,17},{17,25},{2,10},{10,18},{18,26},{... | collective-permute-start | bytes 1572872 | tf_op jit(solution)/shard_map/ppermute | solution.py:17
  86.1 1.5 slice.109
  87.7 1.6 copy.16
  89.3 10.2 %collective-permute-done.1 = f32[256,512]{0,1:T(8,128)S(1)} collective-permute-done((f32[256,512]{0,1:T(8,128)S(1)}, f32[256,512]{0,1:T(8,128)S(1)}, u32[]{:S(2)}, u32[]{:S(2)}) %collective-permute-start.1) | collective-permute-done | bytes 524320 | tf_op jit(solution)/shard_map/ppermute | solution.py:17
  99.8 0.8 copy-done.3
  100.6 3.5 %conditional.7 = (f32[256,512]{0,1:T(8,128)}, f32[1024,512]{0,1:T(8,128)S(1)}, f32[1024,512]{0,1:T(8,128)S(1)}) conditional(s32[]{:T(128)} %convert_element_type.22, (s32[]{:T(128)}, f32[1024,512]{0,1:T(8,128)S(1)}, f32[256,256]{1,0:T(8,128)}, f32[512,256]{1,0:T(8,128)S(1)}) %tuple.142, (f32[512,512]{0,1:T(8,128)}, f32[1024,512]{0,1:T(8,128)S(1)}) %tuple.88), branch_computations={%region_4.5_spmd, %region_5.6_spmd} | conditional | flops 2013659392 | bytes 12847222 | solution.py:78
  100.9 1.9 slice.91
  102.8 1.3 pad_maximum_fusion.1
  104.1 1.3 copy-done.6
  105.4 0.8 slice.118
  106.2 1.9 collective-permute-start.2
  108.8 12.8 %collective-permute-done.2 = f32[256,512]{0,1:T(8,128)S(1)} collective-permute-done((f32[256,512]{0,1:T(8,128)}, f32[256,512]{0,1:T(8,128)S(1)}, u32[]{:S(2)}, u32[]{:S(2)}) %collective-permute-start.2) | collective-permute-done | bytes 524320 | tf_op jit(solution)/shard_map/ppermute | solution.py:17
  121.6 2.4 %conditional.8 = (f32[512,512]{0,1:T(8,128)}, f32[256,512]{0,1:T(8,128)S(1)}) conditional(s32[]{:T(128)} %convert_element_type.21, (f32[256,512]{0,1:T(8,128)}, f32[256,512]{0,1:T(8,128)S(1)}) %tuple.89, (f32[256,512]{0,1:T(8,128)}, f32[256,512]{0,1:T(8,128)S(1)}, f32[256,256]{1,0:T(8,128)S(1)}, f32[512,256]{1,0:T(8,128)S(1)}) %tuple.145), branch_computations={%region_8.9_spmd, %region_9.10_spmd} | conditional | flops 2013659392 | bytes 9701392 | solution.py:53
  121.6 2.2 %pad_maximum_fusion.2 = f32[512,512]{0,1:T(8,128)} fusion(f32[256,512]{0,1:T(8,128)S(1)} %get-tuple-element.252, f32[256,512]{0,1:T(8,128)} %get-tuple-element.160), kind=kLoop, calls=%fused_computation.26 | loop fusion | flops 262144 | bytes 2097152 | tf_op jit(solution)/shard_map/cond/branch_0_fun/concatenate | solution.py:58
  124.1 3.6 %collective-permute-start.3 = (f32[256,512]{0,1:T(8,128)S(1)}, f32[256,512]{0,1:T(8,128)S(1)}, u32[]{:S(2)}, u32[]{:S(2)}) collective-permute-start(f32[256,512]{0,1:T(8,128)S(1)} %broadcast_select_fusion.1), channel_id=1, source_target_pairs={{0,8},{8,16},{16,24},{1,9},{9,17},{17,25},{2,10},{10,18},{18,26},{... | collective-permute-start | bytes 1572872 | tf_op jit(solution)/shard_map/ppermute | solution.py:17
  127.8 11.7 %collective-permute-done.3 = f32[256,512]{0,1:T(8,128)S(1)} collective-permute-done((f32[256,512]{0,1:T(8,128)S(1)}, f32[256,512]{0,1:T(8,128)S(1)}, u32[]{:S(2)}, u32[]{:S(2)}) %collective-permute-start.3) | collective-permute-done | bytes 524320 | tf_op jit(solution)/shard_map/ppermute | solution.py:17
  139.6 1.1 broadcast_select_fusion.4
  140.9 0.8 copy-done.2
  141.7 5.3 %conditional.9 = (f32[256,512]{0,1:T(8,128)}, f32[1024,512]{0,1:T(8,128)S(1)}, f32[1024,512]{0,1:T(8,128)S(1)}) conditional(s32[]{:T(128)} %convert_element_type.21, (s32[]{:T(128)}, f32[1024,512]{0,1:T(8,128)S(1)}, f32[256,256]{1,0:T(8,128)}, f32[512,256]{1,0:T(8,128)S(1)}) %tuple.141, (f32[512,512]{0,1:T(8,128)}, ...), branch_computations={%region_10.11_spmd, %region_11.12_spmd} | conditional | flops 2013659392 | bytes 12847222 | solution.py:78
  142.4 1.0 fusion.24
  143.5 0.6 fusion.26
  144.1 1.9 fusion.23
  146.2 0.8 slice.123
  147.0 1.3 copy-done.7
  148.3 0.8 slice.119
  149.2 1.9 collective-permute-start.4
  151.7 10.9 %collective-permute-done.4 = f32[256,512]{0,1:T(8,128)S(1)} collective-permute-done((f32[256,512]{0,1:T(8,128)}, f32[256,512]{0,1:T(8,128)S(1)}, u32[]{:S(2)}, u32[]{:S(2)}) %collective-permute-start.4) | collective-permute-done | bytes 524320 | tf_op jit(solution)/shard_map/ppermute | solution.py:17
  162.7 2.5 %conditional.10 = (f32[512,512]{0,1:T(8,128)}, f32[256,512]{0,1:T(8,128)S(1)}) conditional(s32[]{:T(128)} %convert_element_type.20, (f32[256,512]{0,1:T(8,128)}, f32[256,512]{0,1:T(8,128)S(1)}) %tuple.93, (f32[256,512]{0,1:T(8,128)}, f32[256,512]{0,1:T(8,128)S(1)}, f32[256,256]{1,0:T(8,128)S(1)}, f32[512,256]{1,0:T(8,128)S(1)}) %tuple.143), branch_computations={%region_14.15_spmd, %region_15.16_spmd} | conditional | flops 2013659392 | bytes 9701392 | solution.py:53
  162.7 2.2 %pad_maximum_fusion.4 = f32[512,512]{0,1:T(8,128)} fusion(f32[256,512]{0,1:T(8,128)S(1)} %get-tuple-element.262, f32[256,512]{0,1:T(8,128)} %get-tuple-element.172), kind=kLoop, calls=%fused_computation.52 | loop fusion | flops 262144 | bytes 2097152 | tf_op jit(solution)/shard_map/cond/branch_0_fun/concatenate | solution.py:58
  165.2 1.9 %collective-permute-start.5 = (f32[256,512]{0,1:T(8,128)S(1)}, f32[256,512]{0,1:T(8,128)S(1)}, u32[]{:S(2)}, u32[]{:S(2)}) collective-permute-start(f32[256,512]{0,1:T(8,128)S(1)} %broadcast_select_fusion.2), channel_id=1, source_target_pairs={{0,8},{8,16},{16,24},{1,9},{9,17},{17,25},{2,10},{10,18},{18,26},{... | collective-permute-start | bytes 1572872 | tf_op jit(solution)/shard_map/ppermute | solution.py:17
  167.3 10.4 %collective-permute-done.5 = f32[256,512]{0,1:T(8,128)S(1)} collective-permute-done((f32[256,512]{0,1:T(8,128)S(1)}, f32[256,512]{0,1:T(8,128)S(1)}, u32[]{:S(2)}, u32[]{:S(2)}) %collective-permute-start.5) | collective-permute-done | bytes 524320 | tf_op jit(solution)/shard_map/ppermute | solution.py:17
  177.6 1.1 broadcast_select_fusion.3
  179.0 6.0 %conditional.11 = (f32[1024,512]{1,0:T(8,128)}) conditional(s32[]{:T(128)} %convert_element_type.20, (s32[]{:T(128)}, f32[1024,512]{0,1:T(8,128)S(1)}, f32[256,256]{1,0:T(8,128)S(1)}, f32[512,256]{1,0:T(8,128)S(1)}) %tuple.144, (f32[1024,512]{0,1:T(8,128)S(1)}, f32[512,512]{0,1:T(8,128)}) %tuple.96), branch_computations={%region_16.17_spmd, %region_17.18_spmd} | conditional | flops 2013659392 | bytes 12582920 | solution.py:78
  179.7 1.0 fusion.40
  181.3 1.9 fusion.39
  183.2 1.8 copy.12
  (48 shorter events, 3.7 us)
Async XLA Ops:
  6.5 5.6 %copy-start.14 = (f32[1,1,256,256]{3,2,1,0:T(8,128)S(1)}, f32[1,1,256,256]{3,2,1,0:T(8,128)}, u32[]{:S(2)}) copy-start(f32[1,1,256,256]{3,2,1,0:T(8,128)} %param.21) | copy-start | bytes 786436
  6.5 71.0 %all-reduce.3.cloned.1.call-start = ((), (), s32[]{:S(2)}) async-start(), calls=%async_computation | async-start | bytes 4718592 | tf_op jit(solution)/shard_map/psum | solution.py:11
  12.2 1.9 copy-start.8
  14.3 15.6 %collective-permute-start = (f32[256,512]{0,1:T(8,128)S(1)}, f32[256,512]{0,1:T(8,128)S(1)}, u32[]{:S(2)}, u32[]{:S(2)}) collective-permute-start(f32[256,512]{0,1:T(8,128)S(1)} %copy.15), channel_id=1, source_target_pairs={{8,0},{16,8},{24,16},{9,1},{17,9},{25,17},{10,2},{18,10},{26,18},{... | collective-permute-start | bytes 1572872 | tf_op jit(solution)/shard_map/ppermute | solution.py:17
  77.5 1.0 copy-start.4
  77.5 2.0 %copy-start.12 = (f32[256,256]{1,0:T(8,128)S(1)}, f32[256,256]{1,0:T(8,128)}, u32[]{:S(2)}) copy-start(f32[256,256]{1,0:T(8,128)} %get-tuple-element.152) | copy-start | bytes 786436 | tf_op jit(solution)/shard_map/cond
  84.2 15.3 %collective-permute-start.1 = (f32[256,512]{0,1:T(8,128)S(1)}, f32[256,512]{0,1:T(8,128)S(1)}, u32[]{:S(2)}, u32[]{:S(2)}) collective-permute-start(f32[256,512]{0,1:T(8,128)S(1)} %broadcast_select_fusion), channel_id=1, source_target_pairs={{0,8},{8,16},{16,24},{1,9},{9,17},{17,25},{2,10},{10,18},{18,26},{... | collective-permute-start | bytes 1572872 | tf_op jit(solution)/shard_map/ppermute | solution.py:17
  89.3 10.3 %copy-start.5 = (f32[768,512]{0,1:T(8,128)S(1)}, f32[768,512]{0,1:T(8,128)}, u32[]{:S(2)}) copy-start(f32[768,512]{0,1:T(8,128)} %copy.16) | copy-start | bytes 4718596
  99.6 1.0 copy-start.3
  100.6 20.9 %copy-start.1 = (f32[512,256]{1,0:T(8,128)S(1)}, f32[512,256]{1,0:T(8,128)}, u32[]{:S(2)}) copy-start(f32[512,256]{1,0:T(8,128)} %get-tuple-element.221) | copy-start | bytes 1572868
  100.6 20.9 %copy-start.10 = (f32[256,256]{1,0:T(8,128)S(1)}, f32[256,256]{1,0:T(8,128)}, u32[]{:S(2)}) copy-start(f32[256,256]{1,0:T(8,128)} %get-tuple-element.220) | copy-start | bytes 786436
  104.1 1.3 copy-start.6
  106.2 15.3 %collective-permute-start.2 = (f32[256,512]{0,1:T(8,128)}, f32[256,512]{0,1:T(8,128)S(1)}, u32[]{:S(2)}, u32[]{:S(2)}) collective-permute-start(f32[256,512]{0,1:T(8,128)} %slice.118), channel_id=1, source_target_pairs={{8,0},{16,8},{24,16},{9,1},{17,9},{25,17},{10,2},{18,10},{26,18},{... | collective-permute-start | bytes 1572872 | tf_op jit(solution)/shard_map/ppermute | solution.py:17
  124.1 15.5 %collective-permute-start.3 = (f32[256,512]{0,1:T(8,128)S(1)}, f32[256,512]{0,1:T(8,128)S(1)}, u32[]{:S(2)}, u32[]{:S(2)}) collective-permute-start(f32[256,512]{0,1:T(8,128)S(1)} %broadcast_select_fusion.1), channel_id=1, source_target_pairs={{0,8},{8,16},{16,24},{1,9},{9,17},{17,25},{2,10},{10,18},{18,26},{... | collective-permute-start | bytes 1572872 | tf_op jit(solution)/shard_map/ppermute | solution.py:17
  140.7 1.0 copy-start.2
  141.7 21.0 %copy-start = (f32[512,256]{1,0:T(8,128)S(1)}, f32[512,256]{1,0:T(8,128)}, u32[]{:S(2)}) copy-start(f32[512,256]{1,0:T(8,128)} %get-tuple-element.223) | copy-start | bytes 1572868
  141.7 21.0 %copy-start.9 = (f32[256,256]{1,0:T(8,128)S(1)}, f32[256,256]{1,0:T(8,128)}, u32[]{:S(2)}) copy-start(f32[256,256]{1,0:T(8,128)} %get-tuple-element.222) | copy-start | bytes 786436
  142.4 1.0 copy-start.11
  147.0 1.3 copy-start.7
  149.2 13.5 %collective-permute-start.4 = (f32[256,512]{0,1:T(8,128)}, f32[256,512]{0,1:T(8,128)S(1)}, u32[]{:S(2)}, u32[]{:S(2)}) collective-permute-start(f32[256,512]{0,1:T(8,128)} %slice.119), channel_id=1, source_target_pairs={{8,0},{16,8},{24,16},{9,1},{17,9},{25,17},{10,2},{18,10},{26,18},{... | collective-permute-start | bytes 1572872 | tf_op jit(solution)/shard_map/ppermute | solution.py:17
  165.2 12.4 %collective-permute-start.5 = (f32[256,512]{0,1:T(8,128)S(1)}, f32[256,512]{0,1:T(8,128)S(1)}, u32[]{:S(2)}, u32[]{:S(2)}) collective-permute-start(f32[256,512]{0,1:T(8,128)S(1)} %broadcast_select_fusion.2), channel_id=1, source_target_pairs={{0,8},{8,16},{16,24},{1,9},{9,17},{17,25},{2,10},{10,18},{18,26},{... | collective-permute-start | bytes 1572872 | tf_op jit(solution)/shard_map/ppermute | solution.py:17
Sparse Core Ops, SparseCore 0:
  13.2 64.2 all-reduce.2
where the time goes:
time: 193 us; the launch traced here: 192 us
  waiting for transfers between devices  116 us (60%)
  local copies, waits for them, and re-layouts  19.2 us (10%)
  between operations  17.4 us (9%)
  starting transfers between devices  13.7 us (7%)
  other arithmetic  12.1 us (6%)
  matrix products  11.6 us (6%)
  loops' own time  1.93 us (1%)
    ppermute x6, waiting for transfers between devices, passed_along(): lax.ppermute(value, axis, [(source, source + steps) for source in range(f...  68.4 us
    psum x1, waiting for transfers between devices, broadcast(): return lax.psum(kept, axis)  47.6 us
    ppermute x6, starting transfers between devices, passed_along(): lax.ppermute(value, axis, [(source, source + steps) for source in range(f...  13.7 us
    unnamed x25, local copies, waits for them, and re-layouts  7.18 us
    dot_general x3, matrix products, apply_reflector_block(): jnp.dot(vector_matrix, mixed_rows, precision=high_precision, preferred_el...  6.68 us
    concatenate x2, other arithmetic, body(): jnp.concatenate([bottom_row, lower_rows], axis=0)  4.39 us
  transfers between devices with their start and end apart: 7, of which 7 were waited for; matrix products, arithmetic and copies ran while one was open for 2% of the time, Pallas kernels for 0%

commit v1 on v0

--- a/solution.py
+++ b/solution.py
@@ -8,7 +8,8 @@
 
 def broadcast(value, axis, source):
     kept = jnp.where(lax.axis_index(axis) == source, value, 0).astype(value.dtype)
-    return lax.psum(kept, axis)
+    note_digits_on = lambda x0, lane_axis: jnp.sum(lax.all_gather(x0, axis_name=lane_axis), axis=0)
+    return note_digits_on(kept, axis)
 
 
 def passed_along(value, axis, steps):

time: 193 us -> 252 us (1.31)
  waiting for transfers between devices: 116 us -> 161 us
  other arithmetic: 12.1 us -> 26.9 us
  local copies, waits for them, and re-layouts: 19.2 us -> 16.2 us
    all_gather x0 -> x6, waiting for transfers between devices: none -> 107 us  [broadcast(): lax.all_gather(x0, axis_name=lane_axis)]
    psum x1 -> x0, waiting for transfers between devices: 47.6 us -> none  [broadcast(): return lax.psum(kept, axis)]
    ppermute x6, waiting for transfers between devices: 68.4 us -> 52.5 us  [passed_along(): lax.ppermute(value, axis, [(source, source + steps) for source in range(f...]
    reduce_sum x0 -> x6, other arithmetic: none -> 12.8 us  [broadcast(): jnp.sum(lax.all_gather(x0, axis_name=lane_axis), axis=0)]
    unnamed x25 -> x11, local copies, waits for them, and re-layouts: 7.18 us -> 5.69 us
  transfers between devices with their start and end apart: 7 -> 12, of which waited for: 7 -> 8; matrix products, arithmetic and copies ran while one was open for 2% -> 16% of each run, Pallas kernels for 0% -> 0%
where the time goes in v1:
time: 252 us; the launch traced here: 250 us
  waiting for transfers between devices  161 us (64%)
  other arithmetic  26.9 us (11%)
  between operations  17.4 us (7%)
  local copies, waits for them, and re-layouts  16.2 us (6%)
  starting transfers between devices  15.1 us (6%)
  matrix products  11.6 us (5%)
    all_gather x6, waiting for transfers between devices, broadcast(): lax.all_gather(x0, axis_name=lane_axis)  107 us
    ppermute x6, waiting for transfers between devices, passed_along(): lax.ppermute(value, axis, [(source, source + steps) for source in range(f...  52.5 us
    ppermute x6, starting transfers between devices, passed_along(): lax.ppermute(value, axis, [(source, source + steps) for source in range(f...  14.9 us
    reduce_sum x6, other arithmetic, broadcast(): jnp.sum(lax.all_gather(x0, axis_name=lane_axis), axis=0)  12.8 us
    dot_general x3, matrix products, apply_reflector_block(): jnp.dot(vector_matrix, mixed_rows, precision=high_precision, preferred_el...  6.71 us
    unnamed x11, local copies, waits for them, and re-layouts  5.69 us
  transfers between devices with their start and end apart: 12, of which 8 were waited for; matrix products, arithmetic and copies ran while one was open for 16% of the time, Pallas kernels for 0%

profile of v1, /device:TPU:12, one launch (start us, length us, event | category | flops | bytes accessed | tf_op | source)
XLA Modules:
  0.0 250.3 jit_solution(202398072631426686)
XLA Ops:
  6.5 1.5 constant_dynamic-slice_fusion.2
  9.8 1.9 broadcast_select_fusion.9
  11.8 2.4 broadcast_select_fusion
  17.6 1.2 copy.19
  18.8 2.4 collective-permute-start
  22.1 12.3 %collective-permute-done = f32[256,512]{0,1:T(8,128)S(1)} collective-permute-done((f32[256,512]{0,1:T(8,128)S(1)}, f32[256,512]{0,1:T(8,128)S(1)}, u32[]{:S(2)}, u32[]{:S(2)}) %collective-permute-start) | collective-permute-done | bytes 524320 | tf_op jit(solution)/shard_map/ppermute | solution.py:18
  34.4 6.3 %all-gather.13.cloned.1.call-done = f32[8,1,256,256]{3,2,1,0:T(8,128)} async-done(((f32[1,1,256,256]{3,2,1,0:T(8,128)}), f32[8,1,256,256]{3,2,1,0:T(8,128)}) %all-gather.13.cloned.1.call-update) | async-done | bytes 2097168 | tf_op jit(solution)/shard_map/all_gather | solution.py:11
  40.7 1.8 reduce_sum.54
  42.5 36.7 %all-gather.15.cloned.1.call-done = f32[8,1,512,256]{3,2,1,0:T(8,128)} async-done(((f32[1,1,512,256]{3,2,1,0:T(8,128)}), f32[8,1,512,256]{3,2,1,0:T(8,128)}) %all-gather.15.cloned.1.call-update) | async-done | bytes 4194320 | tf_op jit(solution)/shard_map/all_gather | solution.py:11
  79.1 2.5 %reduce_sum.55 = f32[512,256]{1,0:T(8,128)S(1)} reduce(f32[8,1,512,256]{3,2,1,0:T(8,128)} %all-gather.15.cloned.1.call-done, f32[]{:T(128)} %constant.73.clone.1), dimensions={0,1}, to_apply=%region_0.1 | reduce | flops 917504 | bytes 4718596 | tf_op jit(solution)/shard_map/reduce_sum | solution.py:11
  81.6 5.8 %conditional.6 = (f32[512,512]{0,1:T(8,128)}, f32[256,512]{0,1:T(8,128)S(1)}) conditional(s32[]{:T(128)} %convert_element_type.22, (f32[256,512]{0,1:T(8,128)S(1)}, f32[256,512]{0,1:T(8,128)S(1)}) %tuple.85, (f32[256,512]{0,1:T(8,128)S(1)}, f32[256,512]{0,1:T(8,128)S(1)}, f32[256,256]{1,0:T(8,128)S(1)}, f32[512,256]{1,0:T(8,128)S(1)}) %tuple.86), branch_computations={%region_2.3_spmd, %region_3.4_spmd} | conditional | flops 2013659392 | bytes 9701392 | solution.py:54
  81.8 1.0 fusion.49
  83.5 2.9 %fusion = f32[512,512]{0,1:T(8,128)} fusion(f32[512,512]{0,1:T(8,128)S(1)} %constant_dynamic-update-slice_fusion, f32[256,512]{1,0:T(8,128)S(1)} %fusion.1, f32[512,256]{1,0:T(8,128)S(1)} %get-tuple-element.153), kind=kOutput, calls=%fused_computation.2 | convolution fusion | flops 805568512 | bytes 3145728 | tf_op jit(solution)/shard_map/cond/branch_1_fun/dot_general | solution.py:32
  86.4 1.1 slice.120
  87.5 0.9 broadcast_select_fusion.3
  88.3 1.9 collective-permute-start.1
  90.2 1.6 copy.20
  91.9 12.6 %collective-permute-done.1 = f32[256,512]{0,1:T(8,128)S(1)} collective-permute-done((f32[256,512]{0,1:T(8,128)}, f32[256,512]{0,1:T(8,128)S(1)}, u32[]{:S(2)}, u32[]{:S(2)}) %collective-permute-start.1) | collective-permute-done | bytes 524320 | tf_op jit(solution)/shard_map/ppermute | solution.py:18
  104.8 3.5 %conditional.7 = (f32[256,512]{0,1:T(8,128)}, f32[1024,512]{0,1:T(8,128)S(1)}, f32[1024,512]{0,1:T(8,128)S(1)}) conditional(s32[]{:T(128)} %convert_element_type.22, (s32[]{:T(128)}, f32[1024,512]{0,1:T(8,128)S(1)}, f32[256,256]{1,0:T(8,128)S(1)}, f32[512,256]{1,0:T(8,128)S(1)}) %tuple.87, (f32[512,512]{0,1:T(8,128)}, f32[1024,512]{0,1:T(8,128)S(1)}) %tuple.88), branch_computations={%region_4.5_spmd, %region_5.6_spmd} | conditional | flops 2013659392 | bytes 12582936 | solution.py:79
  105.1 1.9 slice.91
  107.0 1.3 pad_maximum_fusion.1
  108.3 1.3 copy-done.2
  110.4 1.9 collective-permute-start.2
  112.9 1.8 reduce_sum.56
  114.7 32.5 %all-gather.19.cloned.1.call-done = f32[8,1,512,256]{3,2,1,0:T(8,128)} async-done(((f32[1,1,512,256]{3,2,1,0:T(8,128)}), f32[8,1,512,256]{3,2,1,0:T(8,128)}) %all-gather.19.cloned.1.call-update) | async-done | bytes 4194320 | tf_op jit(solution)/shard_map/all_gather | solution.py:11
  147.2 2.5 %reduce_sum.57 = f32[512,256]{1,0:T(8,128)S(1)} reduce(f32[8,1,512,256]{3,2,1,0:T(8,128)} %all-gather.19.cloned.1.call-done, f32[]{:T(128)} %constant.73.clone.1), dimensions={0,1}, to_apply=%region_6.7 | reduce | flops 917504 | bytes 4718596 | tf_op jit(solution)/shard_map/reduce_sum | solution.py:11
  149.7 2.5 conditional.8
  149.7 2.2 pad_maximum_fusion.2
  152.3 3.4 %collective-permute-start.3 = (f32[256,512]{0,1:T(8,128)S(1)}, f32[256,512]{0,1:T(8,128)S(1)}, u32[]{:S(2)}, u32[]{:S(2)}) collective-permute-start(f32[256,512]{0,1:T(8,128)S(1)} %broadcast_select_fusion.4), channel_id=1, source_target_pairs={{0,8},{8,16},{16,24},{1,9},{9,17},{17,25},{2,10},{10,18},{18,26},{... | collective-permute-start | bytes 1572872 | tf_op jit(solution)/shard_map/ppermute | solution.py:18
  155.8 15.2 %collective-permute-done.3 = f32[256,512]{0,1:T(8,128)S(1)} collective-permute-done((f32[256,512]{0,1:T(8,128)S(1)}, f32[256,512]{0,1:T(8,128)S(1)}, u32[]{:S(2)}, u32[]{:S(2)}) %collective-permute-start.3) | collective-permute-done | bytes 524320 | tf_op jit(solution)/shard_map/ppermute | solution.py:18
  171.0 1.1 broadcast_select_fusion.7
  172.3 5.1 %conditional.9 = (f32[256,512]{0,1:T(8,128)}, f32[1024,512]{0,1:T(8,128)S(1)}, f32[1024,512]{0,1:T(8,128)S(1)}) conditional(s32[]{:T(128)} %convert_element_type.21, (s32[]{:T(128)}, f32[1024,512]{0,1:T(8,128)S(1)}, f32[256,256]{1,0:T(8,128)S(1)}, f32[512,256]{1,0:T(8,128)S(1)}) %tuple.91, (f32[512,512]{0,1:T(8,128)}, ...), branch_computations={%region_10.11_spmd, %region_11.12_spmd} | conditional | flops 2013659392 | bytes 12582936 | solution.py:79
  172.9 1.0 fusion.24
  174.6 1.9 fusion.23
  177.5 1.3 copy-done.3
  179.6 1.9 collective-permute-start.4
  182.2 1.8 reduce_sum.58
  183.9 31.2 %all-gather.23.cloned.1.call-done = f32[8,1,512,256]{3,2,1,0:T(8,128)} async-done(((f32[1,1,512,256]{3,2,1,0:T(8,128)}), f32[8,1,512,256]{3,2,1,0:T(8,128)}) %all-gather.23.cloned.1.call-update) | async-done | bytes 4194320 | tf_op jit(solution)/shard_map/all_gather | solution.py:11
  215.1 2.5 %reduce_sum.59 = f32[512,256]{1,0:T(8,128)S(1)} reduce(f32[8,1,512,256]{3,2,1,0:T(8,128)} %all-gather.23.cloned.1.call-done, f32[]{:T(128)} %constant.73.clone.1), dimensions={0,1}, to_apply=%region_12.13 | reduce | flops 917504 | bytes 4718596 | tf_op jit(solution)/shard_map/reduce_sum | solution.py:11
  217.6 2.5 conditional.10
  217.6 2.2 pad_maximum_fusion.4
  220.1 3.4 %collective-permute-start.5 = (f32[256,512]{0,1:T(8,128)S(1)}, f32[256,512]{0,1:T(8,128)S(1)}, u32[]{:S(2)}, u32[]{:S(2)}) collective-permute-start(f32[256,512]{0,1:T(8,128)S(1)} %broadcast_select_fusion.5), channel_id=1, source_target_pairs={{0,8},{8,16},{16,24},{1,9},{9,17},{17,25},{2,10},{10,18},{18,26},{... | collective-permute-start | bytes 1572872 | tf_op jit(solution)/shard_map/ppermute | solution.py:18
  223.7 12.4 %collective-permute-done.5 = f32[256,512]{0,1:T(8,128)S(1)} collective-permute-done((f32[256,512]{0,1:T(8,128)S(1)}, f32[256,512]{0,1:T(8,128)S(1)}, u32[]{:S(2)}, u32[]{:S(2)}) %collective-permute-start.5) | collective-permute-done | bytes 524320 | tf_op jit(solution)/shard_map/ppermute | solution.py:18
  236.1 1.1 broadcast_select_fusion.6
  237.5 6.0 %conditional.11 = (f32[1024,512]{1,0:T(8,128)}) conditional(s32[]{:T(128)} %convert_element_type.20, (s32[]{:T(128)}, f32[1024,512]{0,1:T(8,128)S(1)}, f32[256,256]{1,0:T(8,128)S(1)}, f32[512,256]{1,0:T(8,128)S(1)}) %tuple.95, (f32[1024,512]{0,1:T(8,128)S(1)}, f32[512,512]{0,1:T(8,128)}) %tuple.96), branch_computations={%region_16.17_spmd, %region_17.18_spmd} | conditional | flops 2013659392 | bytes 12582920 | solution.py:79
  238.0 1.0 fusion.40
  239.7 1.9 fusion.39
  241.6 1.8 copy.16
  (50 shorter events, 9.9 us)
Async XLA Ops:
  6.5 34.2 %all-gather.13.cloned.1.call-start = ((), (), s32[]{:S(2)}) async-start(), calls=%async_computation | async-start | bytes 2359296 | tf_op jit(solution)/shard_map/all_gather | solution.py:11
  11.7 5.0 %copy-start = (f32[1024,512]{1,0:T(8,128)S(1)}, f32[1024,512]{1,0:T(8,128)}, u32[]{:S(2)}) copy-start(f32[1024,512]{1,0:T(8,128)} %param.17) | copy-start | bytes 6291460
  11.7 67.4 %all-gather.15.cloned.1.call-start = ((), (), s32[]{:S(2)}) async-start(), calls=%async_computation.1 | async-start | bytes 4718592 | tf_op jit(solution)/shard_map/all_gather | solution.py:11
  14.2 98.7 %all-gather.17.cloned.1.call-start = ((), (), s32[]{:S(2)}) async-start(), calls=%async_computation.2 | async-start | bytes 2359296 | tf_op jit(solution)/shard_map/all_gather | solution.py:11
  14.9 132.2 %all-gather.19.cloned.1.call-start = ((), (), s32[]{:S(2)}) async-start(), calls=%async_computation.3 | async-start | bytes 4718592 | tf_op jit(solution)/shard_map/all_gather | solution.py:11
  15.5 166.6 %all-gather.21.cloned.1.call-start = ((), (), s32[]{:S(2)}) async-start(), calls=%async_computation.4 | async-start | bytes 2359296 | tf_op jit(solution)/shard_map/all_gather | solution.py:11
  16.1 199.0 %all-gather.23.cloned.1.call-start = ((), (), s32[]{:S(2)}) async-start(), calls=%async_computation.5 | async-start | bytes 4718592 | tf_op jit(solution)/shard_map/all_gather | solution.py:11
  18.8 15.6 %collective-permute-start = (f32[256,512]{0,1:T(8,128)S(1)}, f32[256,512]{0,1:T(8,128)S(1)}, u32[]{:S(2)}, u32[]{:S(2)}) collective-permute-start(f32[256,512]{0,1:T(8,128)S(1)} %copy.19), channel_id=1, source_target_pairs={{8,0},{16,8},{24,16},{9,1},{17,9},{25,17},{10,2},{18,10},{26,18},{... | collective-permute-start | bytes 1572872 | tf_op jit(solution)/shard_map/ppermute | solution.py:18
  87.4 2.8 %slice-start = ((f32[1024,512]{1,0:T(8,128)}), f32[768,512]{1,0:T(8,128)S(1)}, s32[]{:S(2)}) async-start(f32[1024,512]{1,0:T(8,128)} %param.17), calls=%async_computation.6 | async-start | bytes 3145728 | tf_op jit(solution)/shard_map/slice | solution.py:64
  88.3 16.1 %collective-permute-start.1 = (f32[256,512]{0,1:T(8,128)}, f32[256,512]{0,1:T(8,128)S(1)}, u32[]{:S(2)}, u32[]{:S(2)}) collective-permute-start(f32[256,512]{0,1:T(8,128)} %broadcast_select_fusion.3), channel_id=1, source_target_pairs={{0,8},{8,16},{16,24},{1,9},{9,17},{17,25},{2,10},{10,18},{18,26},{... | collective-permute-start | bytes 1572872 | tf_op jit(solution)/shard_map/ppermute | solution.py:18
  91.9 12.7 %copy-start.1 = (f32[768,512]{0,1:T(8,128)S(1)}, f32[768,512]{0,1:T(8,128)}, u32[]{:S(2)}) copy-start(f32[768,512]{0,1:T(8,128)} %copy.20) | copy-start | bytes 4718596
  108.3 1.3 copy-start.2
  110.4 39.3 %collective-permute-start.2 = (f32[256,512]{0,1:T(8,128)}, f32[256,512]{0,1:T(8,128)S(1)}, u32[]{:S(2)}, u32[]{:S(2)}) collective-permute-start(f32[256,512]{0,1:T(8,128)} %slice.118), channel_id=1, source_target_pairs={{8,0},{16,8},{24,16},{9,1},{17,9},{25,17},{10,2},{18,10},{26,18},{... | collective-permute-start | bytes 1572872 | tf_op jit(solution)/shard_map/ppermute | solution.py:18
  152.3 18.7 %collective-permute-start.3 = (f32[256,512]{0,1:T(8,128)S(1)}, f32[256,512]{0,1:T(8,128)S(1)}, u32[]{:S(2)}, u32[]{:S(2)}) collective-permute-start(f32[256,512]{0,1:T(8,128)S(1)} %broadcast_select_fusion.4), channel_id=1, source_target_pairs={{0,8},{8,16},{16,24},{1,9},{9,17},{17,25},{2,10},{10,18},{18,26},{... | collective-permute-start | bytes 1572872 | tf_op jit(solution)/shard_map/ppermute | solution.py:18
  177.5 1.3 copy-start.3
  179.6 38.0 %collective-permute-start.4 = (f32[256,512]{0,1:T(8,128)}, f32[256,512]{0,1:T(8,128)S(1)}, u32[]{:S(2)}, u32[]{:S(2)}) collective-permute-start(f32[256,512]{0,1:T(8,128)} %slice.119), channel_id=1, source_target_pairs={{8,0},{16,8},{24,16},{9,1},{17,9},{25,17},{10,2},{18,10},{26,18},{... | collective-permute-start | bytes 1572872 | tf_op jit(solution)/shard_map/ppermute | solution.py:18
  220.1 16.0 %collective-permute-start.5 = (f32[256,512]{0,1:T(8,128)S(1)}, f32[256,512]{0,1:T(8,128)S(1)}, u32[]{:S(2)}, u32[]{:S(2)}) collective-permute-start(f32[256,512]{0,1:T(8,128)S(1)} %broadcast_select_fusion.5), channel_id=1, source_target_pairs={{0,8},{8,16},{16,24},{1,9},{9,17},{17,25},{2,10},{10,18},{18,26},{... | collective-permute-start | bytes 1572872 | tf_op jit(solution)/shard_map/ppermute | solution.py:18
Sparse Core Ops, SparseCore 0:
  11.8 28.8 all-gather.12
  42.6 36.4 all-gather.14
  81.0 27.8 all-gather.16
  110.6 36.4 all-gather.18
  148.9 27.8 all-gather.20
  178.5 36.4 all-gather.22
